TPU v7x, 32 devices: a whole 2x2x4 slice. The times are simulated.
32 devices in a mesh: seq: 8 (over y, x, core), mp: 4 (over z).
Axes of the slice: x: 2, y: 2, z: 4, core: 2. Of those that a mesh axis runs over, the one named last changes fastest.
Arguments:
- frames: bfloat16 [192, 250, 256], P('seq'), may hold values from -7.5 to 7.5
- intra_qkv: bfloat16 [256, 3, 256], P(None, None, 'mp'), may hold values from -20 to 20
- intra_out: bfloat16 [256, 256], P('mp'), may hold values from -0.375 to 0.375
- intra_up: bfloat16 [256, 1024], P(None, 'mp'), may hold values from -0.375 to 0.375
- intra_down: bfloat16 [1024, 256], P('mp'), may hold values from -0.1875 to 0.1875
- inter_qkv: bfloat16 [256, 3, 256], P(None, None, 'mp'), may hold values from -20 to 20
- inter_out: bfloat16 [256, 256], P('mp'), may hold values from -0.375 to 0.375
- inter_up: bfloat16 [256, 1024], P(None, 'mp'), may hold values from -0.375 to 0.375
- inter_down: bfloat16 [1024, 256], P('mp'), may hold values from -0.1875 to 0.1875
Outputs:
- margin_sum: bfloat16 [24000, 256], P('seq')
All inputs are finite; a program needn't handle non-finite values.
Results may differ from a plain program's by a relative error of at most 0.014.
Values may be sent and summed in bfloat16 or wider, within the bound.
A program may use at most 128 MiB of HBM per device.

v0:
```python
import jax
import jax.numpy as jnp
from jax import lax
from jax.sharding import PartitionSpec as P

HEADS = 8
HD = 32
K = 250


def passed_along(shard, axis, by):
    peers = lax.axis_size(axis)
    pairs = [(i, i + by) for i in range(peers) if 0 <= i + by < peers]
    return lax.ppermute(shard, axis, pairs)


def layer_norm(values):
    values = values.astype(jnp.float32)
    centre = values - jnp.mean(values, axis=-1, keepdims=True)
    spread = jnp.mean(centre * centre, axis=-1, keepdims=True)
    return (centre * lax.rsqrt(spread + 1e-05)).astype(jnp.bfloat16)


def attend(query_rows, key_rows, value_rows):
    factor = query_rows.shape[-1] ** (-0.5)
    scores = (
        jnp.einsum("bqhe,bkhe->bhqk", query_rows, key_rows, preferred_element_type=jnp.float32)
        * factor
    )
    scores = scores - jnp.max(scores, axis=-1, keepdims=True)
    weights = jnp.exp(scores)
    weights = (weights / jnp.sum(weights, axis=-1, keepdims=True)).astype(jnp.bfloat16)
    return jnp.einsum(
        "bhqk,bkhe->bqhe", weights, value_rows, preferred_element_type=jnp.float32
    ).astype(jnp.bfloat16)


def attend_rows(query_rows, key_rows, value_rows, per_step):
    blocks = query_rows.shape[0] // per_step
    stacked = tuple(
        (
            member.reshape((blocks, per_step) + member.shape[1:])
            for member in (query_rows, key_rows, value_rows)
        )
    )
    attended = lax.map(lambda pieces: attend(pieces[0], pieces[1], pieces[2]), stacked)
    return attended.reshape(query_rows.shape)


def whole_block(stream, qkv_weight, out_weight, up_weight, down_weight):
    normed = layer_norm(stream)
    projected = jnp.einsum(
        "pcd,dtj->tpcj", normed, qkv_weight, preferred_element_type=jnp.float32
    ).astype(jnp.bfloat16)
    projected = projected.reshape(3, stream.shape[0], stream.shape[1], HEADS, HD)
    attended = attend_rows(projected[0], projected[1], projected[2], 1)
    branch = jnp.einsum(
        "pche,hed->pcd",
        attended,
        out_weight.reshape(HEADS, HD, -1),
        preferred_element_type=jnp.float32,
    )
    middle = (stream.astype(jnp.float32) + branch).astype(jnp.bfloat16)
    normed = layer_norm(middle)
    hidden = jax.nn.relu(
        jnp.einsum("pcd,df->pcf", normed, up_weight, preferred_element_type=jnp.float32)
    ).astype(jnp.bfloat16)
    branch = jnp.einsum("pcf,fd->pcd", hidden, down_weight, preferred_element_type=jnp.float32)
    return (middle.astype(jnp.float32) + branch).astype(jnp.bfloat16)


def on_device(
    frames, intra_qkv, intra_out, intra_up, intra_down, inter_qkv, inter_out, inter_up, inter_down
):
    seq_count = lax.axis_size("seq")
    model_count = lax.axis_size("mp")
    intra_full = (
        lax.all_gather(intra_qkv, "mp", axis=2, tiled=True),
        lax.all_gather(intra_out, "mp", axis=0, tiled=True),
        lax.all_gather(intra_up, "mp", axis=1, tiled=True),
        lax.all_gather(intra_down, "mp", axis=0, tiled=True),
    )
    span_count = frames.shape[0] // model_count
    own_spans = lax.dynamic_slice_in_dim(frames, lax.axis_index("mp") * span_count, span_count, 0)
    finished = whole_block(own_spans, intra_full[0], intra_full[1], intra_full[2], intra_full[3])
    stream = lax.all_gather(finished, "mp", axis=0, tiled=True)
    spread_devices = seq_count * model_count
    padded_len = (K + spread_devices - 1) // spread_devices * spread_devices
    full_weights = (
        lax.all_gather(inter_qkv, "mp", axis=2, tiled=True),
        lax.all_gather(inter_out, "mp", axis=0, tiled=True),
        lax.all_gather(inter_up, "mp", axis=1, tiled=True),
        lax.all_gather(inter_down, "mp", axis=0, tiled=True),
    )
    per_device = padded_len // spread_devices
    arranged = jnp.pad(jnp.transpose(stream, (1, 0, 2)), ((0, padded_len - K), (0, 0), (0, 0)))
    arranged = arranged.reshape(
        seq_count, model_count, per_device, stream.shape[0], stream.shape[2]
    )
    mine = lax.dynamic_index_in_dim(arranged, lax.axis_index("mp"), 1, keepdims=False)
    mine = mine.reshape(seq_count * per_device, stream.shape[0], stream.shape[2])
    spread_rows = lax.all_to_all(mine, "seq", split_axis=0, concat_axis=1, tiled=True)
    spread_rows = whole_block(
        spread_rows, full_weights[0], full_weights[1], full_weights[2], full_weights[3]
    )
    returned = lax.all_to_all(spread_rows, "seq", split_axis=1, concat_axis=0, tiled=True)
    returned = returned.reshape(seq_count, 1, per_device, stream.shape[0], stream.shape[2])
    collected = lax.all_gather(returned, "mp", axis=1, tiled=True)
    collected = collected.reshape(padded_len, stream.shape[0], stream.shape[2])
    stream = jnp.transpose(collected[:K], (1, 0, 2))
    hop_len = K // 2
    tail_rows = stream[:, hop_len:]
    carried = passed_along(tail_rows[-1], "seq", 1)
    earlier = jnp.concatenate([carried[None], tail_rows[:-1]], axis=0)
    summed = stream[:, :hop_len].astype(jnp.float32) + earlier.astype(jnp.float32)
    return summed.astype(jnp.bfloat16).reshape(-1, stream.shape[2])


def solution(mesh):
    return jax.shard_map(
        on_device,
        mesh=mesh,
        in_specs=(
            P("seq", None, None),
            P(None, None, "mp"),
            P("mp", None),
            P(None, "mp"),
            P("mp", None),
            P(None, None, "mp"),
            P("mp", None),
            P(None, "mp"),
            P("mp", None),
        ),
        out_specs=P("seq", None),
        check_vma=False,
    )
```

profile of v0, /device:TPU:4, one launch (start us, length us, event | category | flops | bytes accessed | tf_op | source)
XLA Modules:
  0.0 418.6 jit_solution(934940214543586257)
XLA Ops:
  9.6 14.8 %all_gather.30 = bf16[256,3,256]{0,2,1:T(8,128)(2,1)S(1)} all-gather(bf16[256,3,64]{0,2,1:T(8,128)(2,1)S(1)} %copy-done.7), channel_id=1, replica_groups=mesh['seq'=8,'mp'=4] {'mp'}, dimensions={2}, use_global_device_ids=true | all-gather | bytes 491520 | tf_op jit(solution)/shard_map/all_gather | solution.py:78
  33.7 27.5 %while.20 = (s32[]{:T(128)}, bf16[6,1,250,8,32]{2,4,3,1,0:T(8,128)(2,1)}, bf16[6,1,250,8,32]{2,4,3,1,0:T(8,128)(2,1)}, bf16[6,1,250,8,32]{2,4,3,1,0:T(8,128)(2,1...) while((s32[]{:T(128)}, bf16[6,1,250,8,32]{2,4,3,1,0:T(8,128)(2,1)}, bf16[6,1,250,8,32]{2,4,3,1,0:T(8,128)(2,1)}, ...), condition=%wide.region_5.6_spmd, body=%wide.region_2.5_spmd.sunk | while | flops 99566496 | bytes 805573 | solution.py:46
  35.6 2.7 fusion.164
  40.2 2.7 fusion.164
  44.8 2.7 fusion.164
  49.3 2.8 fusion.164
  53.9 2.7 fusion.164
  58.5 2.7 fusion.164
  61.3 13.8 %all_gather.31 = bf16[256,256]{1,0:T(8,128)(2,1)S(1)} all-gather(bf16[64,256]{1,0:T(8,128)(2,1)S(1)} %copy-done.8), channel_id=1, replica_groups=mesh['seq'=8,'mp'=4] {'mp'}, dimensions={0}, use_global_device_ids=true | all-gather | bytes 163840 | tf_op jit(solution)/shard_map/all_gather | solution.py:79
  78.5 16.5 %all_gather.32 = bf16[256,1024]{1,0:T(8,128)(2,1)} all-gather(bf16[256,256]{1,0:T(8,128)(2,1)S(1)} %copy-done.4), channel_id=1, replica_groups=mesh['seq'=8,'mp'=4] {'mp'}, dimensions={1}, use_global_device_ids=true | all-gather | bytes 655360 | tf_op jit(solution)/shard_map/all_gather | solution.py:80
  95.0 15.7 %all_gather.33 = bf16[1024,256]{1,0:T(8,128)(2,1)} all-gather(bf16[256,256]{1,0:T(8,128)(2,1)S(1)} %copy-done.5), channel_id=1, replica_groups=mesh['seq'=8,'mp'=4] {'mp'}, dimensions={0}, use_global_device_ids=true | all-gather | bytes 655360 | tf_op jit(solution)/shard_map/all_gather | solution.py:81
  110.7 4.5 %fusion.94 = bf16[6,250,256]{2,1,0:T(8,128)(2,1)} fusion(bf16[6,250,256]{2,1,0:T(8,128)(2,1)} %copy-done.3, f32[6,250]{1,0:T(8,128)S(1)} %add_rsqrt_fusion.2, f32[6,250]{1,0:T(8,128)S(1)} %broadcast_multiply_fusion.2, bf16[1024,256]{1,0:T(8,128)(2,1)} %all_gather.33, bf16[256,1024]{1,0:T(8,128)(2,1)} %all_gather.32), kind=kOutput, calls=%fused_computation.84 | convolution fusion | flops 1578624000 | bytes 2596576 | tf_op jit(solution)/shard_map/pcf,fd->pcd/dot_general | solution.py:68
  115.3 65.1 %all-gather.4.cloned.1.call-done = bf16[24,250,256]{2,1,0:T(8,128)(2,1)} async-done(((bf16[6,250,256]{2,1,0:T(8,128)(2,1)}), bf16[24,250,256]{2,1,0:T(8,128)(2,1)}) %all-gather.4.cloned.1.call-update) | async-done | bytes 3072016 | tf_op jit(solution)/shard_map/all_gather | solution.py:86
  184.1 4.7 %all-to-all-start = ((bf16[64,24,256]{2,1,0:T(8,128)(2,1)}), bf16[64,24,256]{2,1,0:T(8,128)(2,1)}, u32[]{:S(2)}, u32[]{:S(2)}) async-start(bf16[64,24,256]{2,1,0:T(8,128)(2,1)} %bitcast.194), calls=%async_computation | async-start | bytes 1572864 | tf_op jit(solution)/shard_map/all_to_all | solution.py:102
  188.8 14.3 %all_gather.36 = bf16[256,256]{1,0:T(8,128)(2,1)} all-gather(bf16[64,256]{1,0:T(8,128)(2,1)S(1)} %copy-done.9), channel_id=1, replica_groups=mesh['seq'=8,'mp'=4] {'mp'}, dimensions={0}, use_global_device_ids=true | all-gather | bytes 163840 | tf_op jit(solution)/shard_map/all_gather | solution.py:91
  203.1 14.5 %all_gather.35 = bf16[256,3,256]{0,2,1:T(8,128)(2,1)S(1)} all-gather(bf16[256,3,64]{0,2,1:T(8,128)(2,1)} %param.18), channel_id=1, replica_groups=mesh['seq'=8,'mp'=4] {'mp'}, dimensions={2}, use_global_device_ids=true | all-gather | bytes 491520 | tf_op jit(solution)/shard_map/all_gather | solution.py:90
  217.6 16.9 %all_gather.37 = bf16[256,1024]{1,0:T(8,128)(2,1)} all-gather(bf16[256,256]{1,0:T(8,128)(2,1)} %param.20), channel_id=1, replica_groups=mesh['seq'=8,'mp'=4] {'mp'}, dimensions={1}, use_global_device_ids=true | all-gather | bytes 655360 | tf_op jit(solution)/shard_map/all_gather | solution.py:92
  234.5 15.8 %all_gather.38 = bf16[1024,256]{1,0:T(8,128)(2,1)} all-gather(bf16[256,256]{1,0:T(8,128)(2,1)} %param.21), channel_id=1, replica_groups=mesh['seq'=8,'mp'=4] {'mp'}, dimensions={0}, use_global_device_ids=true | all-gather | bytes 655360 | tf_op jit(solution)/shard_map/all_gather | solution.py:93
  267.2 41.7 %while.21 = (s32[]{:T(128)}, bf16[8,1,192,8,32]{2,4,3,1,0:T(8,128)(2,1)}, bf16[8,1,192,8,32]{2,4,3,1,0:T(8,128)(2,1)}, bf16[8,1,192,8,32]{2,4,3,1,0:T(8,128)(2,1...) while((s32[]{:T(128)}, bf16[8,1,192,8,32]{2,4,3,1,0:T(8,128)(2,1)}, ...), condition=%wide.region_13.14_spmd, body=%wide.region_10.13_spmd.sunk | while | flops 39272640 | bytes 3291205 | solution.py:46
  267.2 2.8 fusion.168
  272.4 2.8 fusion.168
  277.6 2.8 fusion.168
  282.9 2.8 fusion.168
  288.1 2.8 fusion.168
  293.3 2.8 fusion.168
  298.5 2.8 fusion.168
  303.7 2.8 fusion.168
  312.7 4.5 %fusion.95 = bf16[8,192,256]{2,1,0:T(8,128)(2,1)} fusion(bf16[8,192,256]{2,1,0:T(8,128)(2,1)} %copy-done.2, f32[8,192]{1,0:T(8,128)S(1)} %add_rsqrt_fusion.1, f32[8,192]{1,0:T(8,128)S(1)} %broadcast_multiply_fusion.1, bf16[1024,256]{1,0:T(8,128)(2,1)} %all_gather.38, bf16[256,1024]{1,0:T(8,128)(2,1)} %all_gather.37), kind=kOutput, calls=%fused_computation.85 | convolution fusion | flops 1616510976 | bytes 2633728 | tf_op jit(solution)/shard_map/pcf,fd->pcd/dot_general | solution.py:68
  318.8 15.1 %all_to_all.24 = bf16[8,192,256]{2,0,1:T(8,128)(2,1)S(1)} all-to-all(bf16[8,192,256]{2,0,1:T(8,128)(2,1)S(1)} %copy.150), channel_id=1, replica_groups=mesh['seq'=8,'mp'=4] {'seq'}, dimensions={1} | all-to-all | bytes 1572864 | tf_op jit(solution)/shard_map/all_to_all | solution.py:106
  334.9 62.6 %all-gather.6.cloned.1.call-done = bf16[8,32,24,256]{3,2,0,1:T(8,128)(2,1)} async-done(((bf16[8,8,24,256]{3,2,0,1:T(8,128)(2,1)}), bf16[8,32,24,256]{3,2,0,1:T(8,128)(2,1)}) %all-gather.6.cloned.1.call-update) | async-done | bytes 3145744 | tf_op jit(solution)/shard_map/all_gather | solution.py:108
  402.0 4.4 %collective-permute-done = bf16[125,256]{1,0:T(8,128)(2,1)S(1)} collective-permute-done((bf16[125,256]{1,0:T(8,128)(2,1)S(1)}, bf16[125,256]{1,0:T(8,128)(2,1)S(1)}, u32[]{:S(2)}, u32[]{:S(2)}) %collective-permute-start) | collective-permute-done | bytes 64032 | tf_op jit(solution)/shard_map/ppermute | solution.py:14
  409.1 2.7 reshape.186
  (90 shorter events, 80.0 us)
Async XLA Ops:
  6.5 1.9 copy-start
  6.5 173.9 %all-gather.4.cloned.1.call-start = ((), (), s32[]{:S(2)}) async-start(), calls=%async_computation.2 | async-start | bytes 3932160 | tf_op jit(solution)/shard_map/all_gather | solution.py:86
  8.4 1.2 copy-start.7
  8.7 16.7 %copy-start.1 = (bf16[6,250,256]{2,0,1:T(8,128)(2,1)}, bf16[6,250,256]{2,0,1:T(8,128)(2,1)S(1)}, u32[]{:S(2)}) copy-start(bf16[6,250,256]{2,0,1:T(8,128)(2,1)S(1)} %constant_dynamic-slice_fusion.1) | copy-start | bytes 2304004
  33.7 27.5 %copy-start.8 = (bf16[64,256]{1,0:T(8,128)(2,1)S(1)}, bf16[64,256]{1,0:T(8,128)(2,1)}, u32[]{:S(2)}) copy-start(bf16[64,256]{1,0:T(8,128)(2,1)} %param.15) | copy-start | bytes 98308
  75.1 3.4 copy-start.4
  77.1 0.9 copy-start.3
  77.1 17.9 %copy-start.5 = (bf16[256,256]{1,0:T(8,128)(2,1)S(1)}, bf16[256,256]{1,0:T(8,128)(2,1)}, u32[]{:S(2)}) copy-start(bf16[256,256]{1,0:T(8,128)(2,1)} %param.17) | copy-start | bytes 393220
  182.8 6.0 %copy-start.9 = (bf16[64,256]{1,0:T(8,128)(2,1)S(1)}, bf16[64,256]{1,0:T(8,128)(2,1)}, u32[]{:S(2)}) copy-start(bf16[64,256]{1,0:T(8,128)(2,1)} %param.19) | copy-start | bytes 98308
  184.1 66.2 %all-to-all-start = ((bf16[64,24,256]{2,1,0:T(8,128)(2,1)}), bf16[64,24,256]{2,1,0:T(8,128)(2,1)}, u32[]{:S(2)}, u32[]{:S(2)}) async-start(bf16[64,24,256]{2,1,0:T(8,128)(2,1)} %bitcast.194), calls=%async_computation | async-start | bytes 1572864 | tf_op jit(solution)/shard_map/all_to_all | solution.py:102
  188.8 208.7 %all-gather.6.cloned.1.call-start = ((), (), s32[]{:S(2)}) async-start(), calls=%async_computation.3 | async-start | bytes 3932160 | tf_op jit(solution)/shard_map/all_gather | solution.py:108
  267.2 41.7 %copy-start.6 = (bf16[256,256]{1,0:T(8,128)(2,1)S(1)}, bf16[256,256]{1,0:T(8,128)(2,1)}, u32[]{:S(2)}) copy-start(bf16[256,256]{1,0:T(8,128)(2,1)} %all_gather.36) | copy-start | bytes 393220
  311.2 0.9 copy-start.2
  399.9 6.5 %collective-permute-start = (bf16[125,256]{1,0:T(8,128)(2,1)S(1)}, bf16[125,256]{1,0:T(8,128)(2,1)S(1)}, u32[]{:S(2)}, u32[]{:S(2)}) collective-permute-start(bf16[125,256]{1,0:T(8,128)(2,1)S(1)} %bitcast.204), channel_id=1, source_target_pairs={{0,4},{4,8},{8,12},{12,16},{16,20},{20,24},{24,28},{1,5},{5,9},{9,... | collective-permute-start | bytes 192008 | tf_op jit(solution)/shard_map/ppermute | solution.py:14
Sparse Core Ops, SparseCore 0:
  115.4 64.9 all-gather.3
  335.0 62.4 all-gather.5
where the time goes:
time: 420 us; the launch traced here: 419 us
  blocking collectives  137 us (33%)
  waiting for transfers between devices  132 us (31%)
  matrix products  84.4 us (20%)
  local copies, waits for them, and re-layouts  34.7 us (8%)
  between operations  13.7 us (3%)
  other arithmetic  9.62 us (2%)
  starting transfers between devices  6.58 us (2%)
    all_gather x1, waiting for transfers between devices, on_device(): stream = lax.all_gather(finished, 'mp', axis=0, tiled=True)  65.1 us
    all_gather x1, waiting for transfers between devices, on_device(): collected = lax.all_gather(returned, 'mp', axis=1, tiled=True)  62.6 us
    dot_general x14, matrix products, attend(): jnp.einsum('bhqk,bkhe->bqhe', weights, value_rows, preferred_element_type...  35.7 us
    sub x14, matrix products, attend(): scores = scores - jnp.max(scores, axis=-1, keepdims=True)  33.5 us
    all_gather x1, blocking collectives, on_device(): lax.all_gather(inter_up, 'mp', axis=1, tiled=True)  16.9 us
    slice x8, local copies, waits for them, and re-layouts, whole_block(): attended = attend_rows(projected[0], projected[1], projected[2], 1)  16.6 us
    all_gather x1, blocking collectives, on_device(): lax.all_gather(intra_up, 'mp', axis=1, tiled=True)  16.5 us
    all_gather x1, blocking collectives, on_device(): lax.all_gather(inter_down, 'mp', axis=0, tiled=True)  15.8 us
  transfers between devices with their start and end apart: 4, of which 3 were waited for; matrix products, arithmetic and copies ran while one was open for 0% of the time, Pallas kernels for 0%

commit v1 on v0

--- a/solution.py
+++ b/solution.py
@@ -105,7 +105,12 @@
     )
     returned = lax.all_to_all(spread_rows, "seq", split_axis=1, concat_axis=0, tiled=True)
     returned = returned.reshape(seq_count, 1, per_device, stream.shape[0], stream.shape[2])
-    collected = lax.all_gather(returned, "mp", axis=1, tiled=True)
+    ring = [returned]
+    for hop in range(3):
+        ring.append(lax.ppermute(ring[-1], "mp", [(dev, (dev + 1) % 4) for dev in range(4)]))
+    collected = jnp.roll(
+        jnp.concatenate(ring[::-1], axis=1), (lax.axis_index("mp") + 1) * ring[0].shape[1], axis=1
+    )
     collected = collected.reshape(padded_len, stream.shape[0], stream.shape[2])
     stream = jnp.transpose(collected[:K], (1, 0, 2))
     hop_len = K // 2

time: 420 us -> 396 us (0.943)
  local copies, waits for them, and re-layouts: 34.7 us -> 22.8 us
  waiting for transfers between devices: 132 us -> 127 us
  other arithmetic: 9.62 us -> 4.79 us
  matrix products: 84.4 us -> 79.9 us
    all_gather x1 -> x0, waiting for transfers between devices: 62.6 us -> none  [on_device(): collected = lax.all_gather(returned, 'mp', axis=1, tiled=True)]
    ppermute x0 -> x3, waiting for transfers between devices: none -> 58.7 us  [on_device(): lax.ppermute(ring[-1], 'mp', [(dev, (dev + 1) % 4) for dev in range(4)])]
    slice x8, local copies, waits for them, and re-layouts: 16.6 us -> 9.81 us  [whole_block(): attended = attend_rows(projected[0], projected[1], projected[2], 1)]
  transfers between devices with their start and end apart: 4 -> 6, of which waited for: 3 -> 5; matrix products, arithmetic and copies ran while one was open for 0% -> 0% of each run, Pallas kernels for 0% -> 0%
where the time goes in v1:
time: 396 us; the launch traced here: 393 us
  blocking collectives  139 us (35%)
  waiting for transfers between devices  127 us (32%)
  matrix products  79.9 us (20%)
  local copies, waits for them, and re-layouts  22.8 us (6%)
  between operations  13.8 us (3%)
  starting transfers between devices  6.59 us (2%)
  other arithmetic  4.79 us (1%)
    all_gather x1, waiting for transfers between devices, on_device(): stream = lax.all_gather(finished, 'mp', axis=0, tiled=True)  63.6 us
    ppermute x3, waiting for transfers between devices, on_device(): lax.ppermute(ring[-1], 'mp', [(dev, (dev + 1) % 4) for dev in range(4)])  58.7 us
    dot_general x14, matrix products, attend(): jnp.einsum('bhqk,bkhe->bqhe', weights, value_rows, preferred_element_type...  35.4 us
    sub x14, matrix products, attend(): scores = scores - jnp.max(scores, axis=-1, keepdims=True)  33.3 us
    all_gather x1, blocking collectives, on_device(): lax.all_gather(intra_up, 'mp', axis=1, tiled=True)  17.2 us
    all_gather x1, blocking collectives, on_device(): lax.all_gather(inter_up, 'mp', axis=1, tiled=True)  16.5 us
    all_gather x1, blocking collectives, on_device(): lax.all_gather(intra_down, 'mp', axis=0, tiled=True)  15.8 us
    all_gather x1, blocking collectives, on_device(): lax.all_gather(intra_out, 'mp', axis=0, tiled=True)  15.7 us
  transfers between devices with their start and end apart: 6, of which 5 were waited for; matrix products, arithmetic and copies ran while one was open for 0% of the time, Pallas kernels for 0%

profile of v1, /device:TPU:4, one launch (start us, length us, event | category | flops | bytes accessed | tf_op | source)
XLA Modules:
  0.0 393.5 jit_solution(9650580714763573197)
XLA Ops:
  6.5 15.7 %all_gather.28 = bf16[256,256]{1,0:T(8,128)(2,1)} all-gather(bf16[64,256]{1,0:T(8,128)(2,1)} %param.15), channel_id=1, replica_groups=mesh['seq'=8,'mp'=4] {'mp'}, dimensions={0}, use_global_device_ids=true | all-gather | bytes 163840 | tf_op jit(solution)/shard_map/all_gather | solution.py:79
  22.3 14.8 %all_gather.27 = bf16[256,3,256]{0,2,1:T(8,128)(2,1)S(1)} all-gather(bf16[256,3,64]{0,2,1:T(8,128)(2,1)} %param.14), channel_id=1, replica_groups=mesh['seq'=8,'mp'=4] {'mp'}, dimensions={2}, use_global_device_ids=true | all-gather | bytes 491520 | tf_op jit(solution)/shard_map/all_gather | solution.py:78
  37.1 17.2 %all_gather.29 = bf16[256,1024]{1,0:T(8,128)(2,1)} all-gather(bf16[256,256]{1,0:T(8,128)(2,1)} %param.16), channel_id=1, replica_groups=mesh['seq'=8,'mp'=4] {'mp'}, dimensions={1}, use_global_device_ids=true | all-gather | bytes 655360 | tf_op jit(solution)/shard_map/all_gather | solution.py:80
  54.4 15.8 %all_gather.30 = bf16[1024,256]{1,0:T(8,128)(2,1)} all-gather(bf16[256,256]{1,0:T(8,128)(2,1)} %param.17), channel_id=1, replica_groups=mesh['seq'=8,'mp'=4] {'mp'}, dimensions={0}, use_global_device_ids=true | all-gather | bytes 655360 | tf_op jit(solution)/shard_map/all_gather | solution.py:81
  75.1 26.9 %while.20 = (s32[]{:T(128)}, bf16[6,1,250,8,32]{2,4,3,1,0:T(8,128)(2,1)}, bf16[6,1,250,8,32]{2,4,3,1,0:T(8,128)(2,1)}, bf16[6,1,250,8,32]{2,4,3,1,0:T(8,128)(2,1...) while((s32[]{:T(128)}, bf16[6,1,250,8,32]{2,4,3,1,0:T(8,128)(2,1)}, ...), condition=%wide.region_5.6_spmd, body=%wide.region_2.5_spmd.sunk | while | flops 99566496 | bytes 805773 | solution.py:46
  77.0 2.7 fusion.164
  81.5 2.7 fusion.164
  90.4 2.7 fusion.164
  94.9 2.7 fusion.164
  99.4 2.7 fusion.164
  104.4 2.8 fusion.94
  107.3 63.6 %all-gather.2.cloned.1.call-done = bf16[24,250,256]{2,1,0:T(8,128)(2,1)} async-done(((bf16[6,250,256]{2,1,0:T(8,128)(2,1)}), bf16[24,250,256]{2,1,0:T(8,128)(2,1)}) %all-gather.2.cloned.1.call-update) | async-done | bytes 3072016 | tf_op jit(solution)/shard_map/all_gather | solution.py:86
  174.5 4.2 %all-to-all-start = ((bf16[64,24,256]{2,1,0:T(8,128)(2,1)}), bf16[64,24,256]{2,1,0:T(8,128)(2,1)S(1)}, u32[]{:S(2)}, u32[]{:S(2)}) async-start(bf16[64,24,256]{2,1,0:T(8,128)(2,1)} %bitcast.31), calls=%async_computation | async-start | bytes 1572864 | tf_op jit(solution)/shard_map/all_to_all | solution.py:102
  178.7 13.7 %all_gather.33 = bf16[256,256]{1,0:T(8,128)(2,1)S(1)} all-gather(bf16[64,256]{1,0:T(8,128)(2,1)S(1)} %copy-done.11), channel_id=1, replica_groups=mesh['seq'=8,'mp'=4] {'mp'}, dimensions={0}, use_global_device_ids=true | all-gather | bytes 163840 | tf_op jit(solution)/shard_map/all_gather | solution.py:91
  192.4 14.3 %all_gather.32 = bf16[256,3,256]{0,2,1:T(8,128)(2,1)S(1)} all-gather(bf16[256,3,64]{0,2,1:T(8,128)(2,1)S(1)} %copy-done.10), channel_id=1, replica_groups=mesh['seq'=8,'mp'=4] {'mp'}, dimensions={2}, use_global_device_ids=true | all-gather | bytes 491520 | tf_op jit(solution)/shard_map/all_gather | solution.py:90
  206.7 16.5 %all_gather.34 = bf16[256,1024]{1,0:T(8,128)(2,1)} all-gather(bf16[256,256]{1,0:T(8,128)(2,1)S(1)} %copy-done.7), channel_id=1, replica_groups=mesh['seq'=8,'mp'=4] {'mp'}, dimensions={1}, use_global_device_ids=true | all-gather | bytes 655360 | tf_op jit(solution)/shard_map/all_gather | solution.py:92
  223.2 15.6 %all_gather.35 = bf16[1024,256]{1,0:T(8,128)(2,1)} all-gather(bf16[256,256]{1,0:T(8,128)(2,1)S(1)} %copy-done.8), channel_id=1, replica_groups=mesh['seq'=8,'mp'=4] {'mp'}, dimensions={0}, use_global_device_ids=true | all-gather | bytes 655360 | tf_op jit(solution)/shard_map/all_gather | solution.py:93
  248.5 41.8 %while.21 = (s32[]{:T(128)}, bf16[8,1,192,8,32]{2,4,3,1,0:T(8,128)(2,1)}, bf16[8,1,192,8,32]{2,4,3,1,0:T(8,128)(2,1)}, bf16[8,1,192,8,32]{2,4,3,1,0:T(8,128)(2,1...) while((s32[]{:T(128)}, bf16[8,1,192,8,32]{2,4,3,1,0:T(8,128)(2,1)}, ...), condition=%wide.region_13.14_spmd, body=%wide.region_10.13_spmd.sunk | while | flops 39272640 | bytes 3291213 | solution.py:46
  248.5 2.8 fusion.168
  253.8 2.8 fusion.168
  259.0 2.8 fusion.168
  264.2 2.8 fusion.168
  269.4 2.8 fusion.168
  274.7 2.8 fusion.168
  279.9 2.8 fusion.168
  285.1 2.8 fusion.168
  293.1 3.0 fusion.95
  296.5 15.1 %all_to_all.24 = bf16[8,192,256]{2,0,1:T(8,128)(2,1)S(1)} all-to-all(bf16[8,192,256]{2,0,1:T(8,128)(2,1)S(1)} %copy.126), channel_id=1, replica_groups=mesh['seq'=8,'mp'=4] {'seq'}, dimensions={1} | all-to-all | bytes 1572864 | tf_op jit(solution)/shard_map/all_to_all | solution.py:106
  312.2 20.1 %collective-permute-done = bf16[8,1,8,24,256]{4,3,0,2,1:T(8,128)(2,1)S(1)} collective-permute-done((bf16[8,1,8,24,256]{4,3,0,2,1:T(8,128)(2,1)S(1)}, bf16[8,1,8,24,256]{4,3,0,2,1:T(8,128)(2,1)S(1)}, u32[]{:S(2)}, u32[]{:S(2)}) %collective-permute-start) | collective-permute-done | bytes 786464 | tf_op jit(solution)/shard_map/ppermute | solution.py:110
  332.3 19.7 %collective-permute-done.1 = bf16[8,1,8,24,256]{4,3,0,2,1:T(8,128)(2,1)S(1)} collective-permute-done((bf16[8,1,8,24,256]{4,3,0,2,1:T(8,128)(2,1)S(1)}, bf16[8,1,8,24,256]{4,3,0,2,1:T(8,128)(2,1)S(1)}, u32[]{:S(2)}, u32[]{:S(2)}) %collective-permute-start.1) | collective-permute-done | bytes 786464 | tf_op jit(solution)/shard_map/ppermute | solution.py:110
  352.0 18.9 %collective-permute-done.2 = bf16[8,1,8,24,256]{4,3,0,2,1:T(8,128)(2,1)} collective-permute-done((bf16[8,1,8,24,256]{4,3,0,2,1:T(8,128)(2,1)S(1)}, bf16[8,1,8,24,256]{4,3,0,2,1:T(8,128)(2,1)}, u32[]{:S(2)}, u32[]{:S(2)}) %collective-permute-start.2) | collective-permute-done | bytes 786464 | tf_op jit(solution)/shard_map/ppermute | solution.py:110
  376.8 4.4 %collective-permute-done.3 = bf16[125,256]{1,0:T(8,128)(2,1)S(1)} collective-permute-done((bf16[125,256]{1,0:T(8,128)(2,1)S(1)}, bf16[125,256]{1,0:T(8,128)(2,1)S(1)}, u32[]{:S(2)}, u32[]{:S(2)}) %collective-permute-start.3) | collective-permute-done | bytes 64032 | tf_op jit(solution)/shard_map/ppermute | solution.py:14
  (106 shorter events, 68.1 us)
Async XLA Ops:
  6.5 63.6 %copy-start = (bf16[24,250,256]{2,0,1:T(8,128)(2,1)S(1)}, bf16[24,250,256]{2,0,1:T(8,128)(2,1)}, u32[]{:S(2)}) copy-start(bf16[24,250,256]{2,0,1:T(8,128)(2,1)} %param.13) | copy-start | bytes 9216004
  6.5 164.3 %all-gather.2.cloned.1.call-start = ((), (), s32[]{:S(2)}) async-start(), calls=%async_computation.2 | async-start | bytes 3932160 | tf_op jit(solution)/shard_map/all_gather | solution.py:86
  70.5 1.9 copy-start.2
  75.1 27.0 %copy-start.3 = (bf16[6,250,256]{2,0,1:T(8,128)(2,1)S(1)}, bf16[6,250,256]{2,0,1:T(8,128)(2,1)}, u32[]{:S(2)}) copy-start(bf16[6,250,256]{2,0,1:T(8,128)(2,1)} %copy-done.2) | copy-start | bytes 2304004
  75.1 27.0 %copy-start.9 = (bf16[256,256]{1,0:T(8,128)(2,1)S(1)}, bf16[256,256]{1,0:T(8,128)(2,1)}, u32[]{:S(2)}) copy-start(bf16[256,256]{1,0:T(8,128)(2,1)} %all_gather.28) | copy-start | bytes 393220
  102.1 2.3 copy-start.5
  102.1 2.3 copy-start.6
  173.1 5.7 %copy-start.11 = (bf16[64,256]{1,0:T(8,128)(2,1)S(1)}, bf16[64,256]{1,0:T(8,128)(2,1)}, u32[]{:S(2)}) copy-start(bf16[64,256]{1,0:T(8,128)(2,1)} %param.19) | copy-start | bytes 98308
  173.1 19.3 %copy-start.10 = (bf16[256,3,64]{0,2,1:T(8,128)(2,1)S(1)}, bf16[256,3,64]{0,2,1:T(8,128)(2,1)}, u32[]{:S(2)}) copy-start(bf16[256,3,64]{0,2,1:T(8,128)(2,1)} %param.18) | copy-start | bytes 294916
  173.2 33.5 %copy-start.7 = (bf16[256,256]{1,0:T(8,128)(2,1)S(1)}, bf16[256,256]{1,0:T(8,128)(2,1)}, u32[]{:S(2)}) copy-start(bf16[256,256]{1,0:T(8,128)(2,1)} %param.20) | copy-start | bytes 393220
  173.2 50.0 %copy-start.8 = (bf16[256,256]{1,0:T(8,128)(2,1)S(1)}, bf16[256,256]{1,0:T(8,128)(2,1)}, u32[]{:S(2)}) copy-start(bf16[256,256]{1,0:T(8,128)(2,1)} %param.21) | copy-start | bytes 393220
  174.5 64.3 %all-to-all-start = ((bf16[64,24,256]{2,1,0:T(8,128)(2,1)}), bf16[64,24,256]{2,1,0:T(8,128)(2,1)S(1)}, u32[]{:S(2)}, u32[]{:S(2)}) async-start(bf16[64,24,256]{2,1,0:T(8,128)(2,1)} %bitcast.31), calls=%async_computation | async-start | bytes 1572864 | tf_op jit(solution)/shard_map/all_to_all | solution.py:102
  290.3 2.8 copy-start.4
  311.8 20.6 %collective-permute-start = (bf16[8,1,8,24,256]{4,3,0,2,1:T(8,128)(2,1)S(1)}, bf16[8,1,8,24,256]{4,3,0,2,1:T(8,128)(2,1)S(1)}, u32[]{:S(2)}, u32[]{:S(2)}) collective-permute-start(bf16[8,1,8,24,256]{4,3,0,2,1:T(8,128)(2,1)S(1)} %bitcast.196), channel_id=1, source_target_pairs={{0,1},{1,2},{2,3},{3,0},{4,5},{5,6},{6,7},{7,4},{8,9},{9,10},{10,1... | collective-permute-start | bytes 2359304 | tf_op jit(solution)/shard_map/ppermute | solution.py:110
  332.3 19.7 %collective-permute-start.1 = (bf16[8,1,8,24,256]{4,3,0,2,1:T(8,128)(2,1)S(1)}, bf16[8,1,8,24,256]{4,3,0,2,1:T(8,128)(2,1)S(1)}, u32[]{:S(2)}, u32[]{:S(2)}) collective-permute-start(bf16[8,1,8,24,256]{4,3,0,2,1:T(8,128)(2,1)S(1)} %collective-permute-done), channel_id=1, source_target_pairs={{0,1},{1,2},{2,3},{3,0},{4,5},{5,6},{6,7},{7,4},{8,9},{9,10},{10,1... | collective-permute-start | bytes 2359304 | tf_op jit(solution)/shard_map/ppermute | solution.py:110
  352.0 18.9 %collective-permute-start.2 = (bf16[8,1,8,24,256]{4,3,0,2,1:T(8,128)(2,1)S(1)}, bf16[8,1,8,24,256]{4,3,0,2,1:T(8,128)(2,1)}, u32[]{:S(2)}, u32[]{:S(2)}) collective-permute-start(bf16[8,1,8,24,256]{4,3,0,2,1:T(8,128)(2,1)S(1)} %collective-permute-done.1), channel_id=1, source_target_pairs={{0,1},{1,2},{2,3},{3,0},{4,5},{5,6},{6,7},{7,4},{8,9},{9,10},{10,1... | collective-permute-start | bytes 2359304 | tf_op jit(solution)/shard_map/ppermute | solution.py:110
  374.8 6.5 %collective-permute-start.3 = (bf16[125,256]{1,0:T(8,128)(2,1)S(1)}, bf16[125,256]{1,0:T(8,128)(2,1)S(1)}, u32[]{:S(2)}, u32[]{:S(2)}) collective-permute-start(bf16[125,256]{1,0:T(8,128)(2,1)S(1)} %bitcast.209), channel_id=1, source_target_pairs={{0,4},{4,8},{8,12},{12,16},{16,20},{20,24},{24,28},{1,5},{5,9},{9,... | collective-permute-start | bytes 192008 | tf_op jit(solution)/shard_map/ppermute | solution.py:14
  382.4 4.2 %copy-start.1 = (bf16[24,250,256]{2,0,1:T(8,128)(2,1)S(1)}, bf16[24,250,256]{2,0,1:T(8,128)(2,1)}, u32[]{:S(2)}) copy-start(bf16[24,250,256]{2,0,1:T(8,128)(2,1)} %param.13) | copy-start | bytes 9216004
Sparse Core Ops, SparseCore 0:
  107.4 63.4 all-gather.1
